TPU v7x, 32 devices: a whole 2x2x4 slice. The times are simulated.
32 devices in a mesh: dp: 8 (over y, x, core), mp: 4 (over z).
Axes of the slice: x: 2, y: 2, z: 4, core: 2. Of those that a mesh axis runs over, the one named last changes fastest.
Arguments:
- hidden: bfloat16 [8192, 2048], P('dp'), may hold values from -6 to 6
- cotangent: bfloat16 [8192, 2048], P('dp'), may hold values from -6 to 6
- lengths: int32 [16], P('dp'), may hold values from 64 to 512, as said below
- input_gain: bfloat16 [2048], P('dp'), may hold values from 0.5 to 1.5
- input_shift: bfloat16 [2048], P('dp'), may hold values from -1.25 to 1.25
- triple_weight: bfloat16 [2048, 3, 2048], P('dp', None, 'mp'), may hold values from -0.125 to 0.125
- triple_bias: bfloat16 [2, 2048], P(None, 'mp'), may hold values from -1.25 to 1.25
- merge_weight: bfloat16 [2048, 2048], P('mp', 'dp'), may hold values from -0.5 to 0.5
- merge_bias: bfloat16 [2048], P('dp'), may hold values from -1.25 to 1.25
- middle_gain: bfloat16 [2048], P('dp'), may hold values from 0.5 to 1.5
- middle_shift: bfloat16 [2048], P('dp'), may hold values from -1.25 to 1.25
- expand_weight: bfloat16 [2048, 8192], P('dp', 'mp'), may hold values from -0.125 to 0.125
- expand_bias: bfloat16 [8192], P('mp'), may hold values from -1.25 to 1.25
- reduce_weight: bfloat16 [8192, 2048], P('mp', 'dp'), may hold values from -0.0625 to 0.0625
- reduce_bias: bfloat16 [2048], P('dp'), may hold values from -1.25 to 1.25
Outputs:
- layer_output: bfloat16 [8192, 2048], P('dp')
- hidden_grad: bfloat16 [8192, 2048], P('dp')
- input_gain_grad: float32 [2048], P('dp')
- input_shift_grad: float32 [2048], P('dp')
- triple_weight_grad: float32 [2048, 3, 2048], P('dp', None, 'mp')
- triple_bias_grad: float32 [2, 2048], P(None, 'mp')
- merge_weight_grad: float32 [2048, 2048], P('mp', 'dp')
- merge_bias_grad: float32 [2048], P('dp')
- middle_gain_grad: float32 [2048], P('dp')
- middle_shift_grad: float32 [2048], P('dp')
- expand_weight_grad: float32 [2048, 8192], P('dp', 'mp')
- expand_bias_grad: float32 [8192], P('mp')
- reduce_weight_grad: float32 [8192, 2048], P('mp', 'dp')
- reduce_bias_grad: float32 [2048], P('dp')
- branch_rms: float32 [3], replicated
Inputs may be any that keep to these rules, and one draw needn't show every extreme that they name: `lengths`: each slot's valid tokens stand at its start; in every draw some slot is full (512 valid tokens).
All inputs are finite; a program needn't handle non-finite values.
Results may differ from a plain program's by a relative error of at most 0.023.
Values may be sent and summed in bfloat16 or wider, within the bound.
A program may use at most 256 MiB of HBM per device.

v0:
```python
import jax
import jax.numpy as jnp
from jax import lax
from jax.sharding import PartitionSpec as P

HEADS = 32
HEAD_DIM = 64
SLOT = 512
MICRO = 2


def layer_norm(values, gain_vec, shift_vec):
    center = values - jnp.mean(values, axis=-1, keepdims=True)
    spread = jnp.mean(center * center, axis=-1, keepdims=True)
    return center * lax.rsqrt(spread + 1e-05) * gain_vec + shift_vec


def gelu_exact(values):
    return jax.nn.gelu(values, approximate=False)


def attention_scores(query_low, key_low, slopes, length):
    raw_scores = jnp.einsum("qhe,khe->hqk", query_low, key_low, preferred_element_type=jnp.float32)
    places = jnp.arange(query_low.shape[0], dtype=jnp.int32)
    key_place = places.astype(jnp.float32)
    scores = (raw_scores + slopes[:, None, None] * key_place[None, None, :]) * 0.125
    allowed = (places[None, :] <= places[:, None]) & (places[None, :] < length)
    return jnp.where(allowed[None], scores, -1000000000.0)


def local(
    hidden,
    cotangent,
    lengths,
    input_gain,
    input_shift,
    triple_weight,
    triple_bias,
    merge_weight,
    merge_bias,
    middle_gain,
    middle_shift,
    expand_weight,
    expand_bias,
    reduce_weight,
    reduce_bias,
):
    slot = SLOT
    width = hidden.shape[1]
    head_cols = triple_weight.shape[2]
    unit_cols = expand_weight.shape[1]
    local_heads = head_cols // HEAD_DIM
    head_start = lax.axis_index("mp") * local_heads
    slopes = 2.0 ** (
        -8.0
        * (head_start + jnp.arange(local_heads, dtype=jnp.int32) + 1).astype(jnp.float32)
        / HEADS
    )
    bias_pair = triple_bias.astype(jnp.float32)
    unit_shift = expand_bias.astype(jnp.float32)
    attention_kept = (
        lax.all_gather(input_gain, "dp", axis=0, tiled=True),
        lax.all_gather(input_shift, "dp", axis=0, tiled=True),
        lax.all_gather(triple_weight, "dp", axis=0, tiled=True),
        lax.all_gather(merge_weight, "dp", axis=1, tiled=True),
        lax.all_gather(merge_bias, "dp", axis=0, tiled=True),
    )
    feed_kept = (
        lax.all_gather(middle_gain, "dp", axis=0, tiled=True),
        lax.all_gather(middle_shift, "dp", axis=0, tiled=True),
        lax.all_gather(expand_weight, "dp", axis=0, tiled=True),
        lax.all_gather(reduce_weight, "dp", axis=1, tiled=True),
        lax.all_gather(reduce_bias, "dp", axis=0, tiled=True),
    )
    acc_triple = jnp.zeros((width, 3, head_cols), jnp.float32)
    acc_merge = jnp.zeros((head_cols, width), jnp.float32)
    acc_expand = jnp.zeros((width, unit_cols), jnp.float32)
    acc_reduce = jnp.zeros((unit_cols, width), jnp.float32)
    acc_gain_one = jnp.zeros((width,), jnp.float32)
    acc_shift_one = jnp.zeros((width,), jnp.float32)
    acc_merge_bias = jnp.zeros((width,), jnp.float32)
    acc_gain_two = jnp.zeros((width,), jnp.float32)
    acc_shift_two = jnp.zeros((width,), jnp.float32)
    acc_reduce_bias = jnp.zeros((width,), jnp.float32)
    acc_pair_bias = jnp.zeros((2, head_cols), jnp.float32)
    acc_unit_bias = jnp.zeros((unit_cols,), jnp.float32)
    square_sums = jnp.zeros((4,), jnp.float32)
    output_parts = []
    grad_parts = []
    for batch_index in range(MICRO):
        start = batch_index * slot
        token_rows = hidden[start : start + slot].astype(jnp.float32)
        length = lengths[batch_index]
        valid_rows = (jnp.arange(slot, dtype=jnp.int32) < length)[:, None]
        gain_one, shift_one, triple_full, merge_full, merge_shift = attention_kept
        gain_two, shift_two, expand_full, reduce_full, reduce_shift = feed_kept
        gain_one = gain_one.astype(jnp.float32)
        shift_one = shift_one.astype(jnp.float32)
        gain_two = gain_two.astype(jnp.float32)
        shift_two = shift_two.astype(jnp.float32)
        norm_in = layer_norm(token_rows, gain_one, shift_one).astype(jnp.bfloat16)
        triple = jnp.einsum("td,dcf->tcf", norm_in, triple_full, preferred_element_type=jnp.float32)
        query_low = (
            (triple[:, 0] + bias_pair[0]).astype(jnp.bfloat16).reshape(slot, local_heads, HEAD_DIM)
        )
        key_low = triple[:, 1].astype(jnp.bfloat16).reshape(slot, local_heads, HEAD_DIM)
        value_low = (
            (triple[:, 2] + bias_pair[1]).astype(jnp.bfloat16).reshape(slot, local_heads, HEAD_DIM)
        )
        scores = attention_scores(query_low, key_low, slopes, length)
        log_total = jax.nn.logsumexp(scores, axis=-1)
        attention_weights = jnp.exp(scores - log_total[..., None]).astype(jnp.bfloat16)
        mixed_heads = jnp.einsum(
            "hqk,khe->qhe", attention_weights, value_low, preferred_element_type=jnp.float32
        )
        mixed_heads = mixed_heads.reshape(slot, head_cols).astype(jnp.bfloat16)
        attention_part = jnp.dot(mixed_heads, merge_full, preferred_element_type=jnp.float32)
        attention_branch = lax.psum(attention_part.astype(jnp.bfloat16), "mp").astype(
            jnp.float32
        ) + merge_shift.astype(jnp.float32)
        residual = token_rows + attention_branch
        norm_mid = layer_norm(residual, gain_two, shift_two).astype(jnp.bfloat16)
        token_count = length.astype(jnp.float32)
        expand_pre = jnp.dot(norm_mid, expand_full, preferred_element_type=jnp.float32) + unit_shift
        activation = gelu_exact(expand_pre).astype(jnp.bfloat16)
        feed_part = jnp.dot(activation, reduce_full, preferred_element_type=jnp.float32)
        feed_branch = lax.psum(feed_part.astype(jnp.bfloat16), "mp").astype(
            jnp.float32
        ) + reduce_shift.astype(jnp.float32)
        result = residual + feed_branch
        output_parts.append(jnp.where(valid_rows, result, 0.0).astype(jnp.bfloat16))
        square_sums = square_sums + jnp.stack(
            [
                jnp.sum(jnp.where(valid_rows, result * result, 0.0)),
                jnp.sum(jnp.where(valid_rows, attention_branch * attention_branch, 0.0)),
                jnp.sum(jnp.where(valid_rows, feed_branch * feed_branch, 0.0)),
                token_count,
            ]
        )
        grad_out = jnp.where(valid_rows, cotangent[start : start + slot].astype(jnp.float32), 0.0)
        grad_feed = grad_out.astype(jnp.bfloat16)
        acc_reduce_bias = acc_reduce_bias + jnp.sum(grad_out, axis=0)
        acc_reduce = acc_reduce + jnp.dot(
            activation.T, grad_feed, preferred_element_type=jnp.float32
        )
        grad_act = jnp.dot(grad_feed, reduce_full.T, preferred_element_type=jnp.float32)
        gelu_value, gelu_back = jax.vjp(gelu_exact, expand_pre)
        grad_pre = gelu_back(grad_act)[0].astype(jnp.bfloat16)
        acc_unit_bias = acc_unit_bias + jnp.sum(grad_pre, axis=0, dtype=jnp.float32)
        acc_expand = acc_expand + jnp.dot(norm_mid.T, grad_pre, preferred_element_type=jnp.float32)
        mid_part = jnp.dot(grad_pre, expand_full.T, preferred_element_type=jnp.float32)
        grad_mid = lax.psum(mid_part.astype(jnp.bfloat16), "mp").astype(jnp.float32)
        norm_value, norm_back = jax.vjp(layer_norm, residual, gain_two, shift_two)
        grad_resid_norm, grad_gain_two, grad_shift_two = norm_back(grad_mid)
        acc_gain_two = acc_gain_two + grad_gain_two
        acc_shift_two = acc_shift_two + grad_shift_two
        grad_residual = grad_out + grad_resid_norm
        grad_branch = grad_residual.astype(jnp.bfloat16)
        acc_merge_bias = acc_merge_bias + jnp.sum(grad_branch, axis=0, dtype=jnp.float32)
        acc_merge = acc_merge + jnp.dot(
            mixed_heads.T, grad_branch, preferred_element_type=jnp.float32
        )
        grad_mixed = jnp.dot(grad_branch, merge_full.T, preferred_element_type=jnp.float32)
        grad_mixed = grad_mixed.astype(jnp.bfloat16).reshape(slot, local_heads, HEAD_DIM)
        again_scores = attention_scores(query_low, key_low, slopes, length)
        soft_weights = jnp.exp(again_scores - log_total[..., None])
        grad_probs = jnp.einsum(
            "qhe,khe->hqk", grad_mixed, value_low, preferred_element_type=jnp.float32
        )
        grad_value = jnp.einsum(
            "hqk,qhe->khe",
            soft_weights.astype(jnp.bfloat16),
            grad_mixed,
            preferred_element_type=jnp.float32,
        ).astype(jnp.bfloat16)
        row_terms = jnp.sum(soft_weights * grad_probs, axis=-1, keepdims=True)
        grad_scores = (soft_weights * (grad_probs - row_terms)).astype(jnp.bfloat16)
        grad_query = (
            0.125
            * jnp.einsum("hqk,khe->qhe", grad_scores, key_low, preferred_element_type=jnp.float32)
        ).astype(jnp.bfloat16)
        grad_key = (
            0.125
            * jnp.einsum("hqk,qhe->khe", grad_scores, query_low, preferred_element_type=jnp.float32)
        ).astype(jnp.bfloat16)
        grad_triple = jnp.stack([grad_query, grad_key, grad_value], axis=1).reshape(
            slot, 3, head_cols
        )
        acc_pair_bias = acc_pair_bias + jnp.stack(
            [
                jnp.sum(grad_triple[:, 0], axis=0, dtype=jnp.float32),
                jnp.sum(grad_triple[:, 2], axis=0, dtype=jnp.float32),
            ]
        )
        acc_triple = acc_triple + jnp.einsum(
            "td,tcf->dcf", norm_in, grad_triple, preferred_element_type=jnp.float32
        )
        grad_in_part = jnp.einsum(
            "tcf,dcf->td", grad_triple, triple_full, preferred_element_type=jnp.float32
        )
        grad_in = lax.psum(grad_in_part.astype(jnp.bfloat16), "mp").astype(jnp.float32)
        first_value, first_back = jax.vjp(layer_norm, token_rows, gain_one, shift_one)
        grad_rows_norm, grad_gain_one, grad_shift_one = first_back(grad_in)
        acc_gain_one = acc_gain_one + grad_gain_one
        acc_shift_one = acc_shift_one + grad_shift_one
        input_rows_grad = (grad_residual + grad_rows_norm).astype(jnp.bfloat16)
        grad_parts.append(input_rows_grad)
    owned = (
        lax.psum_scatter(
            acc_triple.astype(jnp.bfloat16), "dp", scatter_dimension=0, tiled=True
        ).astype(jnp.float32),
        lax.psum_scatter(
            acc_merge.astype(jnp.bfloat16), "dp", scatter_dimension=1, tiled=True
        ).astype(jnp.float32),
        lax.psum_scatter(
            acc_expand.astype(jnp.bfloat16), "dp", scatter_dimension=0, tiled=True
        ).astype(jnp.float32),
        lax.psum_scatter(
            acc_reduce.astype(jnp.bfloat16), "dp", scatter_dimension=1, tiled=True
        ).astype(jnp.float32),
        lax.psum_scatter(
            acc_gain_one.astype(jnp.bfloat16), "dp", scatter_dimension=0, tiled=True
        ).astype(jnp.float32),
        lax.psum_scatter(
            acc_shift_one.astype(jnp.bfloat16), "dp", scatter_dimension=0, tiled=True
        ).astype(jnp.float32),
        lax.psum_scatter(
            acc_merge_bias.astype(jnp.bfloat16), "dp", scatter_dimension=0, tiled=True
        ).astype(jnp.float32),
        lax.psum_scatter(
            acc_gain_two.astype(jnp.bfloat16), "dp", scatter_dimension=0, tiled=True
        ).astype(jnp.float32),
        lax.psum_scatter(
            acc_shift_two.astype(jnp.bfloat16), "dp", scatter_dimension=0, tiled=True
        ).astype(jnp.float32),
        lax.psum_scatter(
            acc_reduce_bias.astype(jnp.bfloat16), "dp", scatter_dimension=0, tiled=True
        ).astype(jnp.float32),
    )
    pair_grad, unit_grad, total_sums = lax.psum((acc_pair_bias, acc_unit_bias, square_sums), "dp")
    root_means = jnp.sqrt(total_sums[:3] / (total_sums[3] * width))
    layer_output = jnp.concatenate(output_parts, axis=0)
    hidden_grad = jnp.concatenate(grad_parts, axis=0)
    return (
        layer_output,
        hidden_grad,
        owned[4],
        owned[5],
        owned[0],
        pair_grad,
        owned[1],
        owned[6],
        owned[7],
        owned[8],
        owned[2],
        unit_grad,
        owned[3],
        owned[9],
        root_means,
    )


def solution(mesh):
    return jax.shard_map(
        local,
        mesh=mesh,
        in_specs=(
            P("dp", None),
            P("dp", None),
            P("dp"),
            P("dp"),
            P("dp"),
            P("dp", None, "mp"),
            P(None, "mp"),
            P("mp", "dp"),
            P("dp"),
            P("dp"),
            P("dp"),
            P("dp", "mp"),
            P("mp"),
            P("mp", "dp"),
            P("dp"),
        ),
        out_specs=(
            P("dp", None),
            P("dp", None),
            P("dp"),
            P("dp"),
            P("dp", None, "mp"),
            P(None, "mp"),
            P("mp", "dp"),
            P("dp"),
            P("dp"),
            P("dp"),
            P("dp", "mp"),
            P("mp"),
            P("mp", "dp"),
            P("dp"),
            P(),
        ),
        check_vma=False,
    )
```

profile of v0, /device:TPU:0, one launch (start us, length us, event | category | flops | bytes accessed | tf_op | source)
XLA Modules:
  0.0 1231.0 jit_solution(12049603003931523445)
XLA Ops:
  12.4 3.2 fusion.24
  17.5 10.6 all-gather
  28.1 8.9 all-gather.1
  37.4 22.4 %all-gather.11.cloned.1.call-done = bf16[2048,3,512]{0,2,1:T(8,128)(2,1)} async-done(((bf16[256,3,512]{0,2,1:T(8,128)(2,1)}), bf16[2048,3,512]{0,2,1:T(8,128)(2,1)}) %all-gather.11.cloned.1.call-update) | async-done | bytes 6291472 | tf_op jit(solution)/shard_map/all_gather | solution.py:64
  59.8 6.5 fusion.86
  73.6 16.2 %all-gather.13.cloned.1.call-done = bf16[512,2048]{1,0:T(8,128)(2,1)} async-done(((bf16[512,256]{1,0:T(8,128)(2,1)}), bf16[512,2048]{1,0:T(8,128)(2,1)}) %all-gather.13.cloned.1.call-update) | async-done | bytes 2097168 | tf_op jit(solution)/shard_map/all_gather | solution.py:65
  89.8 4.2 convolution_convert_fusion.5
  94.1 9.3 all-gather.2
  104.3 76.0 %all-reduce.15.cloned.1.call-done = bf16[512,2048]{1,0:T(8,128)(2,1)} async-done(((bf16[512,2048]{1,0:T(8,128)(2,1)}), bf16[512,2048]{1,0:T(8,128)(2,1)}) %all-reduce.15.cloned.1.call-update) | async-done | bytes 2097168 | tf_op jit(solution)/shard_map/psum | solution.py:118
  180.3 4.3 fusion.51
  185.3 5.9 fusion.83
  199.2 2.6 convolution_convert_fusion.3
  203.0 8.9 all-gather.3
  212.0 9.1 all-gather.4
  221.1 66.0 %all-reduce.17.cloned.1.call-done = bf16[512,2048]{1,0:T(8,128)(2,1)} async-done(((bf16[512,2048]{1,0:T(8,128)(2,1)}), bf16[512,2048]{1,0:T(8,128)(2,1)}) %all-reduce.17.cloned.1.call-update) | async-done | bytes 2097168 | tf_op jit(solution)/shard_map/psum | solution.py:118
  287.1 4.0 multiply_reduce_fusion.3
  293.0 49.2 %all-gather.15.cloned.1.call-done = bf16[2048,2048]{1,0:T(8,128)(2,1)} async-done(((bf16[256,2048]{1,0:T(8,128)(2,1)}), bf16[2048,2048]{1,0:T(8,128)(2,1)}) %all-gather.15.cloned.1.call-update) | async-done | bytes 8388624 | tf_op jit(solution)/shard_map/all_gather | solution.py:71
  342.2 8.7 fusion.108
  353.0 26.4 %multiply_convert_fusion.3 = (bf16[512,2048]{1,0:T(8,128)(2,1)}, f32[512,2048]{1,0:T(8,128)}, bf16[512,2048]{1,0:T(8,128)(2,1)}, f32[512,2048]{1,0:T(8,128)}, f32[512,2048]{1,0:T(8,128)}) fusion(f32[2048]{0:T(1024)S(1)} %convert_element_type.369, f32[512,2048]{1,0:T(8,128)S(1)} %fusion.108, bf16[2048,2048]{1,0:T(8,128)(2,1)S(1)} %copy-done.105, ...), kind=kOutput, calls=%fused_computation.120 | convolution fusion | flops 4442816512 | bytes 33591296 | tf_op jit(solution)/shard_map/dot_general | solution.py:124
  379.4 20.4 %all-gather.17.cloned.1.call-done = bf16[2048,2048]{1,0:T(8,128)(2,1)} async-done(((bf16[2048,256]{1,0:T(8,128)(2,1)}), bf16[2048,2048]{1,0:T(8,128)(2,1)}) %all-gather.17.cloned.1.call-update) | async-done | bytes 8388624 | tf_op jit(solution)/shard_map/all_gather | solution.py:72
  399.8 12.9 %convert_reduce_fusion.6 = (f32[2048]{0:T(1024)}, bf16[512,2048]{1,0:T(8,128)(2,1)S(1)}) fusion(f32[512,2048]{1,0:T(8,128)} %get-tuple-element.85, bf16[2048,2048]{1,0:T(8,128)(2,1)} %all-gather.17.cloned.1.call-done, pred[512]{0:T(512)(128)(4,1)S(1)} %iota_compare_fusion.1, bf16[1024,2048]{1,0:T(8,128)(2,1)} %param.16, f32[512,2048]{1,0:T(8,128)} %copy-done.120, ...), kind=kOutput, calls=%fused_computation.81 | convolution fusion | flops 4315936768 | bytes 20988416 | tf_op jit(solution)/shard_map/dot_general | solution.py:146
  412.7 9.9 convolution_convert_fusion
  422.6 11.5 convert_reduce_fusion.7
  434.1 10.0 convolution_convert_fusion.1
  444.1 9.5 convolution_convert_fusion.2
  453.6 5.7 convolution_convert_fusion.4
  460.0 8.9 all-gather.5
  468.9 281.5 %all-reduce.21.cloned.1.call-done = (bf16[512,2048]{1,0:T(8,128)(2,1)}, bf16[512,2048]{1,0:T(8,128)(2,1)}, bf16[512,2048]{1,0:T(8,128)(2,1)}, bf16[512,2048]{1,0:T(8,128)(2,1)}) async-done(((bf16[512,2048]{1,0:T(8,128)(2,1)}, bf16[512,2048]{1,0:T(8,128)(2,1)}, bf16[512,2048]{1,0:T(8,128)(2,1)}, bf16[512,2048]{1,0:T(8,128)(2,1)}), (bf16[512,2048]{1,0:T(8,128)(2,1)}, bf16[512,2048]{1,0:T(8,128)(2,1)}, ...) | async-done | bytes 8388624 | tf_op jit(solution)/shard_map/psum | solution.py:127
  750.5 14.7 %select_reduce_fusion.5 = (f32[]{:T(128)}, f32[512]{0:T(512)S(1)}, f32[512]{0:T(512)S(1)}, f32[]{:T(128)}, f32[]{:T(128)}, /*index=5*/f32[]{:T(128)}, f32[]{:T(1...) fusion(bf16[512,2048]{1,0:T(8,128)(2,1)} %get-tuple-element.67,, ...), kind=kLoop, calls=%fused_computation.80 | loop fusion | flops 55567360 | bytes 25224216 | tf_op jit(solution)/shard_map/reduce_sum | solution.py:134
  765.2 6.0 fusion.30
  771.3 3.6 convert_reduce_fusion.9
  778.2 4.3 multiply_reduce_fusion.1
  782.5 4.5 multiply_convert_fusion.1
  791.5 3.6 convert_reduce_fusion.8
  796.4 4.3 multiply_reduce_fusion
  800.7 2.7 add_convert_fusion.3
  807.6 9.5 multiply_convert_fusion
  817.0 5.5 convert_reduce_fusion.12
  822.8 4.1 convert_reduce_fusion.11
  827.9 3.6 fusion.63
  831.8 5.7 convert_reduce_fusion.10
  838.6 7.5 bitcast_convert_fusion.1
  846.0 7.4 bitcast_convert_fusion
  854.1 13.8 %fusion.106 = f32[2048,2048]{1,0:T(8,128)} fusion(bf16[512,2048]{1,0:T(8,128)(2,1)} %copy-done.119, f32[2048]{0:T(1024)S(1)} %bitcast.180, f32[2048]{0:T(1024)S(1)} %bitcast.161, f32[512]{0:T(512)S(1)} %copy-done.74, bf16[512,2048]{1,0:T(8,128)(2,1)} %all-reduce.15.cloned.1.call-done, f32[512]{0:T(512)S(1)} %broadcast_multiply_fusion.3, ...), kind=kOutput, calls=%fused_computation.249 | convolution fusion | flops 4304404480 | bytes 23097344 | tf_op jit(solution)/shard_map/dot_general | solution.py:150
  867.9 15.6 %add_convert_fusion.1 = bf16[2048,2048]{1,0:T(8,128)(2,1)} fusion(f32[2048,2048]{1,0:T(8,128)} %fusion.106, bf16[512,2048]{1,0:T(8,128)(2,1)} %copy-done.121, f32[512]{0:T(512)S(1)} %copy-done.72, f32[2048]{0:T(1024)S(1)} %bitcast.181, f32[2048]{0:T(1024)S(1)} %bitcast.162, bf16[512,2048]{1,0:T(8,128)(2,1)} %all-reduce.17.cloned.1.call-done, ...), kind=kOutput, calls=%fused_computation.1 | convolution fusion | flops 4312793088 | bytes 31485952 | tf_op jit(solution)/shard_map/dot_general | solution.py:150
  885.0 10.0 fusion.71
  895.0 11.0 add_convert_fusion
  907.4 8.8 fusion.70
  916.2 8.6 add_convert_fusion.2
  928.0 3.9 maximum_add_fusion.1
  931.9 25.5 %all-reduce.6 = (f32[2,512]{1,0:T(2,128)}, f32[2048]{0:T(1024)}, f32[4]{0:T(128)S(1)}) all-reduce(f32[2,512]{1,0:T(2,128)S(1)} %maximum_add_fusion, f32[2048]{0:T(1024)S(1)} %add.360, f32[4]{0:T(128)S(1)} %maximum_add_fusion.1), channel_id=1, replica_groups=mesh['dp'=8,'mp'=4] {'dp'}, use_global_device_ids=true, to_apply=%region_41.42 | all-reduce | flops 3076 | bytes 24608 | tf_op jit(solution)/shard_map/psum | solution.py:240
  959.2 4.1 pad_maximum_fusion
  965.2 42.5 %all-reduce.19.cloned.1.call-done = (bf16[512,2048]{1,0:T(8,128)(2,1)}, bf16[512,2048]{1,0:T(8,128)(2,1)}) async-done(((bf16[512,2048]{1,0:T(8,128)(2,1)}, bf16[512,2048]{1,0:T(8,128)(2,1)}), (bf16[512,2048]{1,0:T(8,128)(2,1)}, bf16[512,2048]{1,0:T(8,128)(2,1)})) %all-reduce.19.cloned.1.call-update) | async-done | bytes 4194320 | tf_op jit(solution)/shard_map/psum | solution.py:201
  1007.6 4.7 fusion.25
  1013.6 4.1 fusion.31
  1017.6 24.3 %all-reduce.7 = (bf16[2048]{0:T(1024)(128)(2,1)S(1)}, bf16[2048]{0:T(1024)(128)(2,1)S(1)}, bf16[2048]{0:T(1024)(128)(2,1)S(1)}, bf16[2048]{0:T(1024)(128)(2,1)S(...) all-reduce(bf16[2048]{0:T(1024)(128)(2,1)S(1)} %add_convert_fusion., ...), channel_id=2, replica_groups=mesh['dp'=8,'mp'=4] {'dp'}, use_global_device_ids=true, to_apply=%region_32.33.clone | all-reduce | flops 12288 | bytes 49152
  1045.9 8.3 add_convert_fusion.6
  1054.2 5.9 add_convert_fusion.4
  1060.1 2.6 pad_maximum_fusion.1
  1062.7 18.8 %reduce-scatter.9.cloned.1.call-done = bf16[256,2048]{1,0:T(8,128)(2,1)} async-done(((bf16[2048,2048]{1,0:T(8,128)(2,1)}), bf16[256,2048]{1,0:T(8,128)(2,1)}) %reduce-scatter.9.cloned.1.call-update) | async-done | bytes 1048592 | tf_op jit(solution)/shard_map/reduce_scatter | solution.py:215
  1081.5 2.8 convert_element_type.446
  1084.3 72.0 %reduce-scatter.11.cloned.1.call-done = bf16[2048,256]{1,0:T(8,128)(2,1)} async-done(((bf16[2048,2048]{1,0:T(8,128)(2,1)}), bf16[2048,256]{1,0:T(8,128)(2,1)}) %reduce-scatter.11.cloned.1.call-update) | async-done | bytes 1048592 | tf_op jit(solution)/shard_map/reduce_scatter | solution.py:218
  1156.3 2.7 convert_element_type.450
  1159.0 62.2 %reduce-scatter.5.cloned.1.call-done = bf16[256,3,512]{2,0,1:T(8,128)(2,1)} async-done(((bf16[2048,3,512]{2,0,1:T(8,128)(2,1)}), bf16[256,3,512]{2,0,1:T(8,128)(2,1)}) %reduce-scatter.5.cloned.1.call-update) | async-done | bytes 786448 | tf_op jit(solution)/shard_map/reduce_scatter | solution.py:209
  (374 shorter events, 60.1 us)
Async XLA Ops:
  7.2 8.9 copy-start.104
  7.2 10.2 copy-start.103
  7.2 10.2 copy-start.109
  7.2 20.8 %copy-start.110 = (bf16[256]{0:T(256)(128)(2,1)S(1)}, bf16[256]{0:T(256)(128)(2,1)}, u32[]{:S(2)}) copy-start(bf16[256]{0:T(256)(128)(2,1)} %param.19) | copy-start | bytes 1540
  7.2 52.6 %all-gather.11.cloned.1.call-start = ((), (), s32[]{:S(2)}) async-start(), calls=%async_computation.4 | async-start | bytes 7077888 | tf_op jit(solution)/shard_map/all_gather | solution.py:64
  9.6 80.3 %all-gather.13.cloned.1.call-start = ((), (), s32[]{:S(2)}) async-start(), calls=%async_computation.5 | async-start | bytes 2359296 | tf_op jit(solution)/shard_map/all_gather | solution.py:65
  10.3 170.0 %all-reduce.15.cloned.1.call-start = ((), (), s32[]{:S(2)}) async-start(), calls=%async_computation.6 | async-start | bytes 4194304 | tf_op jit(solution)/shard_map/psum | solution.py:118
  12.3 54.0 %copy-start.62 = (f32[512]{0:T(512)}, f32[512]{0:T(512)S(1)}, u32[]{:S(2)}) copy-start(f32[512]{0:T(512)S(1)} %broadcast_multiply_fusion.4) | copy-start | bytes 6148
  16.1 50.3 %copy-start.79 = (f32[512]{0:T(512)}, f32[512]{0:T(512)S(1)}, u32[]{:S(2)}) copy-start(f32[512]{0:T(512)S(1)} %fusion.90) | copy-start | bytes 6148
  17.4 753.8 %copy-start.97 = (pred[512]{0:T(512)(128)(4,1)}, pred[512]{0:T(512)(128)(4,1)S(1)}, u32[]{:S(2)}) copy-start(pred[512]{0:T(512)(128)(4,1)S(1)} %iota_compare_fusion.2) | copy-start | bytes 1540
  28.1 156.6 %copy-start.56 = (f32[8,1,256]{2,1,0:T(1,128)}, f32[8,1,256]{2,1,0:T(1,128)S(1)}, u32[]{:S(2)}) copy-start(f32[8,1,256]{2,1,0:T(1,128)S(1)} %convert_element_type.455) | copy-start | bytes 24580
  37.0 147.7 %copy-start.93 = (f32[8,1,256]{2,1,0:T(1,128)}, f32[8,1,256]{2,1,0:T(1,128)S(1)}, u32[]{:S(2)}) copy-start(f32[8,1,256]{2,1,0:T(1,128)S(1)} %convert_element_type.456) | copy-start | bytes 24580
  37.1 154.4 %copy-start.64 = (f32[8,64]{1,0:T(8,128)}, f32[8,64]{1,0:T(8,128)S(1)}, u32[]{:S(2)}) copy-start(f32[8,64]{1,0:T(8,128)S(1)} %add.314) | copy-start | bytes 6148
  37.2 157.8 %copy-start.58 = (f32[8,64]{1,0:T(8,128)}, f32[8,64]{1,0:T(8,128)S(1)}, u32[]{:S(2)}) copy-start(f32[8,64]{1,0:T(8,128)S(1)} %add.311) | copy-start | bytes 6148
  73.6 111.1 %copy-start.39 = (bf16[8,64,512]{2,1,0:T(8,128)(2,1)}, bf16[8,64,512]{2,1,0:T(8,128)(2,1)S(1)}, u32[]{:S(2)}) copy-start(bf16[8,64,512]{2,1,0:T(8,128)(2,1)S(1)} %convolution_convert_fusion.11) | copy-start | bytes 1572868
  73.6 20.5 %copy-start.111 = (bf16[256]{0:T(256)(128)(2,1)S(1)}, bf16[256]{0:T(256)(128)(2,1)}, u32[]{:S(2)}) copy-start(bf16[256]{0:T(256)(128)(2,1)} %param.23) | copy-start | bytes 1540
  94.0 193.1 %all-reduce.17.cloned.1.call-start = ((), (), s32[]{:S(2)}) async-start(), calls=%async_computation.9 | async-start | bytes 4194304 | tf_op jit(solution)/shard_map/psum | solution.py:118
  104.1 646.3 %copy-start.99 = (pred[512]{0:T(512)(128)(4,1)}, pred[512]{0:T(512)(128)(4,1)S(1)}, u32[]{:S(2)}) copy-start(pred[512]{0:T(512)(128)(4,1)S(1)} %iota_compare_fusion.1) | copy-start | bytes 1540
  104.2 87.1 %copy-start.60 = (f32[512]{0:T(512)}, f32[512]{0:T(512)S(1)}, u32[]{:S(2)}) copy-start(f32[512]{0:T(512)S(1)} %broadcast_multiply_fusion.2) | copy-start | bytes 6148
  199.2 12.8 %copy-start.113 = (bf16[256]{0:T(256)(128)(2,1)S(1)}, bf16[256]{0:T(256)(128)(2,1)}, u32[]{:S(2)}) copy-start(bf16[256]{0:T(256)(128)(2,1)} %param.25) | copy-start | bytes 1540
  199.2 21.9 %copy-start.102 = (bf16[2048]{0:T(1024)(128)(2,1)S(1)}, bf16[2048]{0:T(1024)(128)(2,1)}, u32[]{:S(2)}) copy-start(bf16[2048]{0:T(1024)(128)(2,1)} %param.27) | copy-start | bytes 12292
  199.2 88.0 %copy-start.10 = (bf16[512,2048]{1,0:T(8,128)(2,1)S(1)}, bf16[512,2048]{1,0:T(8,128)(2,1)}, u32[]{:S(2)}) copy-start(bf16[512,2048]{1,0:T(8,128)(2,1)} %all-reduce.15.cloned.1.call-done) | copy-start | bytes 6291460
  201.8 140.4 %all-gather.15.cloned.1.call-start = ((), (), s32[]{:S(2)}) async-start(), calls=%async_computation.7 | async-start | bytes 9437184 | tf_op jit(solution)/shard_map/all_gather | solution.py:71
  202.4 197.4 %all-gather.17.cloned.1.call-start = ((), (), s32[]{:S(2)}) async-start(), calls=%async_computation.8 | async-start | bytes 9437184 | tf_op jit(solution)/shard_map/all_gather | solution.py:72
  203.0 547.5 %all-reduce.21.cloned.1.call-start = ((), (), s32[]{:S(2)}) async-start(), calls=%async_computation.15 | async-start | bytes 16777216 | tf_op jit(solution)/shard_map/psum | solution.py:127
  221.0 129.9 %copy-start.95 = (f32[8,1,256]{2,1,0:T(1,128)}, f32[8,1,256]{2,1,0:T(1,128)S(1)}, u32[]{:S(2)}) copy-start(f32[8,1,256]{2,1,0:T(1,128)S(1)} %convert_element_type.459) | copy-start | bytes 24580
  292.9 498.5 %copy-start.71 = (f32[512]{0:T(512)}, f32[512]{0:T(512)S(1)}, u32[]{:S(2)}) copy-start(f32[512]{0:T(512)S(1)} %fusion.93) | copy-start | bytes 6148
  292.9 478.3 %copy-start.73 = (f32[512]{0:T(512)}, f32[512]{0:T(512)S(1)}, u32[]{:S(2)}) copy-start(f32[512]{0:T(512)S(1)} %fusion.91) | copy-start | bytes 6148
  342.2 10.8 copy-start.2
  342.2 10.8 copy-start.105
  412.7 9.9 copy-start.121
  412.7 9.9 copy-start.15
  434.1 10.0 copy-start.119
  434.1 10.0 copy-start.118
  434.1 19.5 %slice-start.4 = ((s8[8388608]{0:T(1024)(128)(4,1)}), s8[4194304]{0:T(1024)(128)(4,1)S(1)}, s32[]{:S(2)}) async-start(s8[8388608]{0:T(1024)(128)(4,1)} %bitcast.182), calls=%async_computation.20 | async-start | bytes 8388608
  444.1 9.5 slice-start.5
  444.1 9.5 copy-start.116
  459.4 504.0 %reduce-scatter.7.cloned.1.call-start = ((), (), s32[]{:S(2)}) async-start(), calls=%async_computation.11 | async-start | bytes 2359296 | tf_op jit(solution)/shard_map/reduce_scatter | solution.py:212
  750.4 14.7 %copy-start.3 = (bf16[1024,2048]{1,0:T(8,128)(2,1)S(1)}, bf16[1024,2048]{1,0:T(8,128)(2,1)}, u32[]{:S(2)}) copy-start(bf16[1024,2048]{1,0:T(8,128)(2,1)} %param.15) | copy-start | bytes 12582916
  750.4 14.7 %copy-start.13 = (bf16[512,2048]{1,0:T(8,128)(2,1)S(1)}, bf16[512,2048]{1,0:T(8,128)(2,1)}, u32[]{:S(2)}) copy-start(bf16[512,2048]{1,0:T(8,128)(2,1)} %all-reduce.17.cloned.1.call-done) | copy-start | bytes 6291460
  750.4 14.7 %copy-start.19 = (bf16[512,2048]{1,0:T(8,128)(2,1)S(1)}, bf16[512,2048]{1,0:T(8,128)(2,1)}, u32[]{:S(2)}) copy-start(bf16[512,2048]{1,0:T(8,128)(2,1)} %get-tuple-element.69) | copy-start | bytes 6291460
  750.4 14.7 %copy-start.21 = (bf16[512,2048]{1,0:T(8,128)(2,1)S(1)}, bf16[512,2048]{1,0:T(8,128)(2,1)}, u32[]{:S(2)}) copy-start(bf16[512,2048]{1,0:T(8,128)(2,1)} %get-tuple-element.68) | copy-start | bytes 6291460
  771.2 20.2 %copy-start.83 = (f32[512]{0:T(512)}, f32[512]{0:T(512)S(1)}, u32[]{:S(2)}) copy-start(f32[512]{0:T(512)S(1)} %get-tuple-element.111) | copy-start | bytes 6148
  803.4 204.2 %all-reduce.19.cloned.1.call-start = ((), (), s32[]{:S(2)}) async-start(), calls=%async_computation.14 | async-start | bytes 8388608 | tf_op jit(solution)/shard_map/psum | solution.py:201
  822.8 15.7 %copy-start.45 = (bf16[512,1,512]{2,0,1:T(8,128)(2,1)}, bf16[512,1,512]{2,0,1:T(8,128)(2,1)S(1)}, u32[]{:S(2)}) copy-start(bf16[512,1,512]{2,0,1:T(8,128)(2,1)S(1)} %copy.57) | copy-start | bytes 1572868
  831.8 14.2 %copy-start.48 = (bf16[512,1,512]{2,0,1:T(8,128)(2,1)}, bf16[512,1,512]{2,0,1:T(8,128)(2,1)S(1)}, u32[]{:S(2)}) copy-start(bf16[512,1,512]{2,0,1:T(8,128)(2,1)S(1)} %copy.63) | copy-start | bytes 1572868
  853.4 14.4 %copy-start.72 = (f32[512]{0:T(512)S(1)}, f32[512]{0:T(512)}, u32[]{:S(2)}) copy-start(f32[512]{0:T(512)} %copy-done.71) | copy-start | bytes 6148
  853.4 228.0 %reduce-scatter.9.cloned.1.call-start = ((), (), s32[]{:S(2)}) async-start(), calls=%async_computation.12 | async-start | bytes 9437184 | tf_op jit(solution)/shard_map/reduce_scatter | solution.py:215
  854.1 13.8 %copy-start.4 = (bf16[1024,2048]{1,0:T(8,128)(2,1)S(1)}, bf16[1024,2048]{1,0:T(8,128)(2,1)}, u32[]{:S(2)}) copy-start(bf16[1024,2048]{1,0:T(8,128)(2,1)} %param.15) | copy-start | bytes 12582916
  883.5 11.6 copy-start.101
  883.5 272.8 %reduce-scatter.11.cloned.1.call-start = ((), (), s32[]{:S(2)}) async-start(), calls=%async_computation.13 | async-start | bytes 9437184 | tf_op jit(solution)/shard_map/reduce_scatter | solution.py:218
  885.0 10.0 copy-start.17
  906.1 10.1 copy-start.49
  906.1 10.1 copy-start.51
  906.1 10.1 copy-start.61
  906.1 10.1 copy-start.82
  906.1 315.1 %reduce-scatter.5.cloned.1.call-start = ((), (), s32[]{:S(2)}) async-start(), calls=%async_computation.10 | async-start | bytes 7077888 | tf_op jit(solution)/shard_map/reduce_scatter | solution.py:209
  924.8 34.3 %copy-start.66 = (f32[2048]{0:T(1024)S(1)}, f32[2048]{0:T(1024)}, u32[]{:S(2)}) copy-start(f32[2048]{0:T(1024)} %get-tuple-element.30) | copy-start | bytes 24580
  924.9 34.3 %copy-start.67 = (f32[2048]{0:T(1024)S(1)}, f32[2048]{0:T(1024)}, u32[]{:S(2)}) copy-start(f32[2048]{0:T(1024)} %get-tuple-element.72) | copy-start | bytes 24580
  924.9 34.3 %copy-start.68 = (f32[2048]{0:T(1024)S(1)}, f32[2048]{0:T(1024)}, u32[]{:S(2)}) copy-start(f32[2048]{0:T(1024)} %get-tuple-element.70) | copy-start | bytes 24580
  924.9 34.3 %copy-start.28 = (bf16[512,2048]{1,0:T(8,128)(2,1)S(1)}, bf16[512,2048]{1,0:T(8,128)(2,1)}, u32[]{:S(2)}) copy-start(bf16[512,2048]{1,0:T(8,128)(2,1)} %get-tuple-element.78) | copy-start | bytes 6291460
  1013.6 32.2 %copy-start.11 = (bf16[512,2048]{1,0:T(8,128)(2,1)S(1)}, bf16[512,2048]{1,0:T(8,128)(2,1)}, u32[]{:S(2)}) copy-start(bf16[512,2048]{1,0:T(8,128)(2,1)} %all-reduce.15.cloned.1.call-done) | copy-start | bytes 6291460
  1013.6 32.2 %copy-start.70 = (f32[512]{0:T(512)S(1)}, f32[512]{0:T(512)}, u32[]{:S(2)}) copy-start(f32[512]{0:T(512)} %copy-done.69) | copy-start | bytes 6148
  1013.6 32.2 %copy-start.86 = (f32[512]{0:T(512)S(1)}, f32[512]{0:T(512)}, u32[]{:S(2)}) copy-start(f32[512]{0:T(512)} %copy-done.85) | copy-start | bytes 6148
  (76 other events, 273.3 us)
Sparse Core Ops, SparseCore 0:
  10.5 49.2 all-gather.10
  61.7 28.0 all-gather.12
  94.2 86.1 all-reduce.14
  201.9 85.1 all-reduce.16
  288.9 53.2 all-gather.14
  343.9 55.8 all-gather.16
  459.5 290.8 all-reduce.20
  803.5 40.1 reduce-scatter.6
  853.5 154.0 all-reduce.18
  1010.9 70.5 reduce-scatter.8
  1084.9 71.2 reduce-scatter.10
  1159.5 61.6 reduce-scatter.4
where the time goes:
time: 1240 us; the launch traced here: 1230 us
  waiting for transfers between devices  729 us (59%)
  matrix products  242 us (20%)
  other arithmetic  108 us (9%)
  blocking collectives  105 us (8%)
  local copies, waits for them, and re-layouts  26.2 us (2%)
  between operations  18.9 us (2%)
    psum x1, waiting for transfers between devices, local(): lax.psum(feed_part.astype(jnp.bfloat16), 'mp').astype(jnp.float32)  282 us
    psum x2, waiting for transfers between devices, local(): lax.psum(attention_part.astype(jnp.bfloat16), 'mp').astype(jnp.float32)  142 us
    reduce_scatter x1, waiting for transfers between devices, local(): lax.psum_scatter(acc_reduce.astype(jnp.bfloat16), 'dp', scatter_dimension...  72 us
    reduce_scatter x1, waiting for transfers between devices, local(): lax.psum_scatter(acc_triple.astype(jnp.bfloat16), 'dp', scatter_dimension...  62.2 us
    all_gather x1, waiting for transfers between devices, local(): lax.all_gather(expand_weight, 'dp', axis=0, tiled=True)  49.2 us
    psum x1, waiting for transfers between devices, local(): lax.psum(grad_in_part.astype(jnp.bfloat16), 'mp').astype(jnp.float32)  42.5 us
    dot_general x2, matrix products, local(): jnp.dot(norm_mid, expand_full, preferred_element_type=jnp.float32)  35.1 us
    dot_general x2, matrix products, local(): jnp.dot(norm_mid.T, grad_pre, preferred_element_type=jnp.float32)  29.3 us
  transfers between devices with their start and end apart: 12, of which 11 were waited for; matrix products, arithmetic and copies ran while one was open for 18% of the time, Pallas kernels for 0%

commit v1 on v0

--- a/solution.py
+++ b/solution.py
@@ -115,7 +115,11 @@
         )
         mixed_heads = mixed_heads.reshape(slot, head_cols).astype(jnp.bfloat16)
         attention_part = jnp.dot(mixed_heads, merge_full, preferred_element_type=jnp.float32)
-        attention_branch = lax.psum(attention_part.astype(jnp.bfloat16), "mp").astype(
+
+        def keep_up_pools(target):
+            return lax.all_gather(target, "mp").sum(axis=0)
+
+        attention_branch = keep_up_pools(attention_part.astype(jnp.bfloat16)).astype(
             jnp.float32
         ) + merge_shift.astype(jnp.float32)
         residual = token_rows + attention_branch

time: 1240 us -> 1340 us (1.081)
  waiting for transfers between devices: 729 us -> 819 us
    all_gather x0 -> x2, waiting for transfers between devices: none -> 268 us  [keep_up_pools(): return lax.all_gather(target, 'mp').sum(axis=0)]
    psum x2 -> x0, waiting for transfers between devices: 142 us -> none  [local(): lax.psum(attention_part.astype(jnp.bfloat16), 'mp').astype(jnp.float32)]
    psum x1, waiting for transfers between devices: 42.5 us -> 155 us  [local(): lax.psum(grad_in_part.astype(jnp.bfloat16), 'mp').astype(jnp.float32)]
    reduce_scatter x1, waiting for transfers between devices: 72 us -> 3.43 us  [local(): lax.psum_scatter(acc_reduce.astype(jnp.bfloat16), 'dp', scatter_dimension...]
    reduce_scatter x1, waiting for transfers between devices: 62.2 us -> 8.59 us  [local(): lax.psum_scatter(acc_triple.astype(jnp.bfloat16), 'dp', scatter_dimension...]
    reduce_scatter x1, waiting for transfers between devices: 18.8 us -> 0.01 us  [local(): lax.psum_scatter(acc_expand.astype(jnp.bfloat16), 'dp', scatter_dimension...]
  transfers between devices with their start and end apart: 12 -> 12, of which waited for: 11 -> 10; matrix products, arithmetic and copies ran while one was open for 18% -> 18% of each run, Pallas kernels for 0% -> 0%
where the time goes in v1:
time: 1340 us; the launch traced here: 1330 us
  waiting for transfers between devices  819 us (61%)
  matrix products  247 us (18%)
  other arithmetic  110 us (8%)
  blocking collectives  106 us (8%)
  local copies, waits for them, and re-layouts  31.1 us (2%)
  between operations  19 us (1%)
    psum x1, waiting for transfers between devices, local(): lax.psum(feed_part.astype(jnp.bfloat16), 'mp').astype(jnp.float32)  282 us
    all_gather x2, waiting for transfers between devices, keep_up_pools(): return lax.all_gather(target, 'mp').sum(axis=0)  268 us
    psum x1, waiting for transfers between devices, local(): lax.psum(grad_in_part.astype(jnp.bfloat16), 'mp').astype(jnp.float32)  155 us
    all_gather x1, waiting for transfers between devices, local(): lax.all_gather(expand_weight, 'dp', axis=0, tiled=True)  40.6 us
    dot_general x2, matrix products, local(): jnp.dot(norm_mid, expand_full, preferred_element_type=jnp.float32)  34.8 us
    dot_general x2, matrix products, local(): jnp.dot(norm_mid.T, grad_pre, preferred_element_type=jnp.float32)  29.7 us
  transfers between devices with their start and end apart: 12, of which 10 were waited for; matrix products, arithmetic and copies ran while one was open for 18% of the time, Pallas kernels for 0%

profile of v1, /device:TPU:0, one launch (start us, length us, event | category | flops | bytes accessed | tf_op | source)
XLA Modules:
  0.0 1333.2 jit_solution(5852620723753710804)
XLA Ops:
  12.4 3.2 fusion.24
  17.5 10.6 all-gather.2
  28.1 8.9 all-gather.3
  37.4 22.4 %all-gather.15.cloned.1.call-done = bf16[2048,3,512]{0,2,1:T(8,128)(2,1)} async-done(((bf16[256,3,512]{0,2,1:T(8,128)(2,1)}), bf16[2048,3,512]{0,2,1:T(8,128)(2,1)}) %all-gather.15.cloned.1.call-update) | async-done | bytes 6291472 | tf_op jit(solution)/shard_map/all_gather | solution.py:64
  59.8 6.5 fusion.86
  73.5 16.3 %all-gather.17.cloned.1.call-done = bf16[512,2048]{1,0:T(8,128)(2,1)} async-done(((bf16[512,256]{1,0:T(8,128)(2,1)}), bf16[512,2048]{1,0:T(8,128)(2,1)}) %all-gather.17.cloned.1.call-update) | async-done | bytes 2097168 | tf_op jit(solution)/shard_map/all_gather | solution.py:65
  89.8 4.2 convolution_convert_fusion.5
  94.1 9.1 all-gather.4
  104.1 139.8 %all-gather.23.cloned.1.call-done = bf16[2048,2048]{1,0:T(8,128)(2,1)} async-done(((bf16[512,2048]{1,0:T(8,128)(2,1)}), bf16[2048,2048]{1,0:T(8,128)(2,1)}) %all-gather.23.cloned.1.call-update) | async-done | bytes 8388624 | tf_op jit(solution)/shard_map/all_gather | solution.py:120
  243.8 5.7 reduce_sum.419
  249.5 4.3 fusion.51
  253.9 5.9 fusion.83
  271.7 9.4 all-gather.5
  281.1 8.9 all-gather.6
  290.1 128.4 %all-gather.25.cloned.1.call-done = bf16[2048,2048]{1,0:T(8,128)(2,1)} async-done(((bf16[512,2048]{1,0:T(8,128)(2,1)}), bf16[2048,2048]{1,0:T(8,128)(2,1)}) %all-gather.25.cloned.1.call-update) | async-done | bytes 8388624 | tf_op jit(solution)/shard_map/all_gather | solution.py:120
  418.5 7.3 reduce_sum.428
  425.7 4.4 multiply_reduce_fusion.3
  432.0 40.6 %all-gather.19.cloned.1.call-done = bf16[2048,2048]{1,0:T(8,128)(2,1)} async-done(((bf16[256,2048]{1,0:T(8,128)(2,1)}), bf16[2048,2048]{1,0:T(8,128)(2,1)}) %all-gather.19.cloned.1.call-update) | async-done | bytes 8388624 | tf_op jit(solution)/shard_map/all_gather | solution.py:71
  472.7 8.7 fusion.108
  483.3 26.1 %multiply_convert_fusion.3 = (bf16[512,2048]{1,0:T(8,128)(2,1)}, f32[512,2048]{1,0:T(8,128)}, bf16[512,2048]{1,0:T(8,128)(2,1)}, f32[512,2048]{1,0:T(8,128)}, f32[512,2048]{1,0:T(8,128)}) fusion(f32[2048]{0:T(1024)S(1)} %convert_element_type.373, f32[512,2048]{1,0:T(8,128)S(1)} %fusion.108, bf16[2048,2048]{1,0:T(8,128)(2,1)S(1)} %copy-done.93, ...), kind=kOutput, calls=%fused_computation.120 | convolution fusion | flops 4442816512 | bytes 33591296 | tf_op jit(solution)/shard_map/dot_general | solution.py:128
  509.4 20.9 %all-gather.21.cloned.1.call-done = bf16[2048,2048]{1,0:T(8,128)(2,1)} async-done(((bf16[2048,256]{1,0:T(8,128)(2,1)}), bf16[2048,2048]{1,0:T(8,128)(2,1)}) %all-gather.21.cloned.1.call-update) | async-done | bytes 8388624 | tf_op jit(solution)/shard_map/all_gather | solution.py:72
  530.3 12.8 convert_reduce_fusion.6
  543.1 9.9 convolution_convert_fusion
  553.0 11.5 convert_reduce_fusion.7
  564.6 10.0 convolution_convert_fusion.1
  574.5 9.5 convolution_convert_fusion.2
  584.1 5.7 convolution_convert_fusion.4
  590.4 8.9 all-gather.7
  599.3 281.5 %all-reduce.15.cloned.1.call-done = (bf16[512,2048]{1,0:T(8,128)(2,1)}, bf16[512,2048]{1,0:T(8,128)(2,1)}, bf16[512,2048]{1,0:T(8,128)(2,1)}, bf16[512,2048]{1,0:T(8,128)(2,1)}) async-done(((bf16[512,2048]{1,0:T(8,128)(2,1)}, bf16[512,2048]{1,0:T(8,128)(2,1)}, bf16[512,2048]{1,0:T(8,128)(2,1)}, bf16[512,2048]{1,0:T(8,128)(2,1)}), (bf16[512,2048]{1,0:T(8,128)(2,1)}, bf16[512,2048]{1,0:T(8,128)(2,1)}, ...) | async-done | bytes 8388624 | tf_op jit(solution)/shard_map/psum | solution.py:131
  880.9 14.7 %select_reduce_fusion.5 = (f32[]{:T(128)}, f32[512]{0:T(512)S(1)}, f32[512]{0:T(512)S(1)}, f32[]{:T(128)}, f32[]{:T(128)}, /*index=5*/f32[]{:T(128)}, f32[]{:T(1...) fusion(bf16[512,2048]{1,0:T(8,128)(2,1)} %get-tuple-element.67,, ...), kind=kLoop, calls=%fused_computation.80 | loop fusion | flops 55567360 | bytes 25224216 | tf_op jit(solution)/shard_map/reduce_sum | solution.py:138
  895.7 5.3 fusion.30
  901.0 2.9 convert_reduce_fusion.9
  904.0 2.9 convert_reduce_fusion.8
  908.3 2.7 add_convert_fusion.3
  911.5 14.0 %fusion.106 = f32[2048,2048]{1,0:T(8,128)} fusion(bf16[512,2048]{1,0:T(8,128)(2,1)} %copy-done.105, f32[2048]{0:T(1024)S(1)} %bitcast.184, f32[2048]{0:T(1024)S(1)} %bitcast.165, f32[512]{0:T(512)S(1)} %fusion.91, bf16[512,2048]{1,0:T(8,128)(2,1)} %copy-done.10, f32[512]{0:T(512)S(1)} %broadcast_multiply_fusion.3, f32[2048]{0:T(1024)S(1)} %bitcast.155, ...), kind=kOutput, calls=%fused_computation.249 | convolution fusion | flops 4304404480 | bytes 23097344 | tf_op jit(solution)/shard_map/dot_general | solution.py:154
  925.5 15.7 %add_convert_fusion.1 = bf16[2048,2048]{1,0:T(8,128)(2,1)} fusion(f32[2048,2048]{1,0:T(8,128)} %fusion.106, bf16[512,2048]{1,0:T(8,128)(2,1)} %copy-done.107, f32[512]{0:T(512)S(1)} %fusion.93, f32[2048]{0:T(1024)S(1)} %bitcast.185, f32[2048]{0:T(1024)S(1)} %bitcast.166, bf16[512,2048]{1,0:T(8,128)(2,1)} %reduce_sum.428, ...), kind=kOutput, calls=%fused_computation.1 | convolution fusion | flops 4312793088 | bytes 31485952 | tf_op jit(solution)/shard_map/dot_general | solution.py:154
  942.8 10.0 fusion.71
  952.8 11.3 add_convert_fusion
  966.0 3.2 convolution_convert_fusion.9
  969.3 5.5 multiply_reduce_fusion.1
  982.3 3.6 fusion.61
  986.8 6.2 convert_reduce_fusion.12
  995.2 2.9 convolution_convert_fusion.7
  998.1 5.1 multiply_reduce_fusion
  1010.1 4.3 fusion.63
  1015.4 5.1 convert_reduce_fusion.10
  1020.8 7.6 bitcast_convert_fusion.1
  1028.4 7.4 bitcast_convert_fusion
  1036.5 10.0 fusion.70
  1046.5 8.7 add_convert_fusion.2
  1058.2 3.9 maximum_add_fusion.1
  1062.2 25.3 %all-reduce.6 = (f32[2,512]{1,0:T(2,128)}, f32[2048]{0:T(1024)}, f32[4]{0:T(128)S(1)}) all-reduce(f32[2,512]{1,0:T(2,128)S(1)} %maximum_add_fusion, f32[2048]{0:T(1024)S(1)} %add.356, f32[4]{0:T(128)S(1)} %maximum_add_fusion.1), channel_id=1, replica_groups=mesh['dp'=8,'mp'=4] {'dp'}, use_global_device_ids=true, to_apply=%region_41.42 | all-reduce | flops 3076 | bytes 24608 | tf_op jit(solution)/shard_map/psum | solution.py:244
  1089.2 4.1 pad_maximum_fusion
  1095.2 2.8 convert_element_type.450
  1098.0 3.4 reduce-scatter.11.cloned.1.call-done
  1101.4 2.7 convert_element_type.454
  1104.1 155.3 %all-reduce.13.cloned.1.call-done = (bf16[512,2048]{1,0:T(8,128)(2,1)}, bf16[512,2048]{1,0:T(8,128)(2,1)}) async-done(((bf16[512,2048]{1,0:T(8,128)(2,1)}, bf16[512,2048]{1,0:T(8,128)(2,1)}), (bf16[512,2048]{1,0:T(8,128)(2,1)}, bf16[512,2048]{1,0:T(8,128)(2,1)})) %all-reduce.13.cloned.1.call-update) | async-done | bytes 4194320 | tf_op jit(solution)/shard_map/psum | solution.py:205
  1259.5 4.7 fusion.25
  1265.4 4.1 fusion.31
  1269.5 24.9 %all-reduce.7 = (bf16[2048]{0:T(1024)(128)(2,1)S(1)}, bf16[2048]{0:T(1024)(128)(2,1)S(1)}, bf16[2048]{0:T(1024)(128)(2,1)S(1)}, bf16[2048]{0:T(1024)(128)(2,1)S(...) all-reduce(bf16[2048]{0:T(1024)(128)(2,1)S(1)} %add_convert_fusion., ...), channel_id=4, replica_groups=mesh['dp'=8,'mp'=4] {'dp'}, use_global_device_ids=true, to_apply=%region_32.33.clone | all-reduce | flops 12288 | bytes 49152
  1298.3 8.0 add_convert_fusion.6
  1306.3 5.9 add_convert_fusion.4
  1312.2 2.6 pad_maximum_fusion.1
  1314.8 8.6 reduce-scatter.5.cloned.1.call-done
  (348 shorter events, 67.7 us)
Async XLA Ops:
  7.2 8.9 copy-start.92
  7.2 10.2 copy-start.91
  7.2 10.2 copy-start.95
  7.2 20.8 %copy-start.96 = (bf16[256]{0:T(256)(128)(2,1)S(1)}, bf16[256]{0:T(256)(128)(2,1)}, u32[]{:S(2)}) copy-start(bf16[256]{0:T(256)(128)(2,1)} %param.19) | copy-start | bytes 1540
  7.2 52.6 %all-gather.15.cloned.1.call-start = ((), (), s32[]{:S(2)}) async-start(), calls=%async_computation.4 | async-start | bytes 7077888 | tf_op jit(solution)/shard_map/all_gather | solution.py:64
  9.6 80.3 %all-gather.17.cloned.1.call-start = ((), (), s32[]{:S(2)}) async-start(), calls=%async_computation.5 | async-start | bytes 2359296 | tf_op jit(solution)/shard_map/all_gather | solution.py:65
  10.3 233.5 %all-gather.23.cloned.1.call-start = ((), (), s32[]{:S(2)}) async-start(), calls=%async_computation.12 | async-start | bytes 10485760 | tf_op jit(solution)/shard_map/all_gather | solution.py:120
  12.3 54.0 %copy-start.64 = (f32[512]{0:T(512)}, f32[512]{0:T(512)S(1)}, u32[]{:S(2)}) copy-start(f32[512]{0:T(512)S(1)} %broadcast_multiply_fusion.4) | copy-start | bytes 6148
  16.1 50.3 %copy-start.76 = (f32[512]{0:T(512)}, f32[512]{0:T(512)S(1)}, u32[]{:S(2)}) copy-start(f32[512]{0:T(512)S(1)} %fusion.90) | copy-start | bytes 6148
  17.4 49.0 %copy-start.88 = (pred[512]{0:T(512)(128)(4,1)}, pred[512]{0:T(512)(128)(4,1)S(1)}, u32[]{:S(2)}) copy-start(pred[512]{0:T(512)(128)(4,1)S(1)} %iota_compare_fusion.2) | copy-start | bytes 1540
  28.1 225.8 %copy-start.58 = (f32[8,1,256]{2,1,0:T(1,128)}, f32[8,1,256]{2,1,0:T(1,128)S(1)}, u32[]{:S(2)}) copy-start(f32[8,1,256]{2,1,0:T(1,128)S(1)} %convert_element_type.459) | copy-start | bytes 24580
  37.0 216.8 %copy-start.86 = (f32[8,1,256]{2,1,0:T(1,128)}, f32[8,1,256]{2,1,0:T(1,128)S(1)}, u32[]{:S(2)}) copy-start(f32[8,1,256]{2,1,0:T(1,128)S(1)} %convert_element_type.460) | copy-start | bytes 24580
  37.1 223.0 %copy-start.66 = (f32[8,64]{1,0:T(8,128)}, f32[8,64]{1,0:T(8,128)S(1)}, u32[]{:S(2)}) copy-start(f32[8,64]{1,0:T(8,128)S(1)} %add.310) | copy-start | bytes 6148
  37.2 226.4 %copy-start.60 = (f32[8,64]{1,0:T(8,128)}, f32[8,64]{1,0:T(8,128)S(1)}, u32[]{:S(2)}) copy-start(f32[8,64]{1,0:T(8,128)S(1)} %add.307) | copy-start | bytes 6148
  73.5 170.3 %copy-start.48 = (bf16[8,64,512]{2,1,0:T(8,128)(2,1)}, bf16[8,64,512]{2,1,0:T(8,128)(2,1)S(1)}, u32[]{:S(2)}) copy-start(bf16[8,64,512]{2,1,0:T(8,128)(2,1)S(1)} %convolution_convert_fusion.11) | copy-start | bytes 1572868
  73.5 20.6 %copy-start.97 = (bf16[256]{0:T(256)(128)(2,1)S(1)}, bf16[256]{0:T(256)(128)(2,1)}, u32[]{:S(2)}) copy-start(bf16[256]{0:T(256)(128)(2,1)} %param.23) | copy-start | bytes 1540
  94.0 324.4 %all-gather.25.cloned.1.call-start = ((), (), s32[]{:S(2)}) async-start(), calls=%async_computation.13 | async-start | bytes 10485760 | tf_op jit(solution)/shard_map/all_gather | solution.py:120
  103.9 150.0 %copy-start.62 = (f32[512]{0:T(512)}, f32[512]{0:T(512)S(1)}, u32[]{:S(2)}) copy-start(f32[512]{0:T(512)S(1)} %broadcast_multiply_fusion.2) | copy-start | bytes 6148
  249.5 651.5 %copy-start.10 = (bf16[512,2048]{1,0:T(8,128)(2,1)}, bf16[512,2048]{1,0:T(8,128)(2,1)S(1)}, u32[]{:S(2)}) copy-start(bf16[512,2048]{1,0:T(8,128)(2,1)S(1)} %reduce_sum.419) | copy-start | bytes 6291460
  253.8 6.0 copy-start.72
  267.9 13.2 copy-start.99
  267.9 22.2 %copy-start.90 = (bf16[2048]{0:T(1024)(128)(2,1)S(1)}, bf16[2048]{0:T(1024)(128)(2,1)}, u32[]{:S(2)}) copy-start(bf16[2048]{0:T(1024)(128)(2,1)} %param.27) | copy-start | bytes 12292
  270.5 202.2 %all-gather.19.cloned.1.call-start = ((), (), s32[]{:S(2)}) async-start(), calls=%async_computation.6 | async-start | bytes 9437184 | tf_op jit(solution)/shard_map/all_gather | solution.py:71
  271.1 259.2 %all-gather.21.cloned.1.call-start = ((), (), s32[]{:S(2)}) async-start(), calls=%async_computation.7 | async-start | bytes 9437184 | tf_op jit(solution)/shard_map/all_gather | solution.py:72
  271.7 609.2 %all-reduce.15.cloned.1.call-start = ((), (), s32[]{:S(2)}) async-start(), calls=%async_computation.15 | async-start | bytes 16777216 | tf_op jit(solution)/shard_map/psum | solution.py:131
  472.7 10.6 copy-start.2
  472.7 10.6 copy-start.93
  543.1 9.9 copy-start.107
  543.1 9.9 copy-start.17
  543.1 9.9 copy-start.89
  564.6 10.0 copy-start.105
  564.6 10.0 copy-start.104
  564.6 19.5 %slice-start.4 = ((s8[8388608]{0:T(1024)(128)(4,1)}), s8[4194304]{0:T(1024)(128)(4,1)S(1)}, s32[]{:S(2)}) async-start(s8[8388608]{0:T(1024)(128)(4,1)} %bitcast.186), calls=%async_computation.20 | async-start | bytes 8388608
  574.5 9.5 slice-start.5
  574.5 9.5 copy-start.102
  589.8 503.6 %reduce-scatter.7.cloned.1.call-start = ((), (), s32[]{:S(2)}) async-start(), calls=%async_computation.9 | async-start | bytes 2359296 | tf_op jit(solution)/shard_map/reduce_scatter | solution.py:216
  880.9 14.8 %copy-start.3 = (bf16[1024,2048]{1,0:T(8,128)(2,1)S(1)}, bf16[1024,2048]{1,0:T(8,128)(2,1)}, u32[]{:S(2)}) copy-start(bf16[1024,2048]{1,0:T(8,128)(2,1)} %param.15) | copy-start | bytes 12582916
  880.9 14.8 %copy-start.13 = (bf16[512,2048]{1,0:T(8,128)(2,1)S(1)}, bf16[512,2048]{1,0:T(8,128)(2,1)}, u32[]{:S(2)}) copy-start(bf16[512,2048]{1,0:T(8,128)(2,1)} %reduce_sum.428) | copy-start | bytes 6291460
  880.9 14.8 %copy-start.21 = (bf16[512,2048]{1,0:T(8,128)(2,1)S(1)}, bf16[512,2048]{1,0:T(8,128)(2,1)}, u32[]{:S(2)}) copy-start(bf16[512,2048]{1,0:T(8,128)(2,1)} %get-tuple-element.69) | copy-start | bytes 6291460
  880.9 14.8 %copy-start.23 = (bf16[512,2048]{1,0:T(8,128)(2,1)S(1)}, bf16[512,2048]{1,0:T(8,128)(2,1)}, u32[]{:S(2)}) copy-start(bf16[512,2048]{1,0:T(8,128)(2,1)} %get-tuple-element.68) | copy-start | bytes 6291460
  895.6 8.3 copy-start.68
  911.0 184.2 %reduce-scatter.9.cloned.1.call-start = ((), (), s32[]{:S(2)}) async-start(), calls=%async_computation.10 | async-start | bytes 9437184 | tf_op jit(solution)/shard_map/reduce_scatter | solution.py:219
  911.5 14.0 %copy-start.4 = (bf16[1024,2048]{1,0:T(8,128)(2,1)S(1)}, bf16[1024,2048]{1,0:T(8,128)(2,1)}, u32[]{:S(2)}) copy-start(bf16[1024,2048]{1,0:T(8,128)(2,1)} %param.15) | copy-start | bytes 12582916
  941.2 160.2 %reduce-scatter.11.cloned.1.call-start = ((), (), s32[]{:S(2)}) async-start(), calls=%async_computation.11 | async-start | bytes 9437184 | tf_op jit(solution)/shard_map/reduce_scatter | solution.py:222
  942.8 10.0 copy-start.19
  964.1 295.4 %all-reduce.13.cloned.1.call-start = ((), (), s32[]{:S(2)}) async-start(), calls=%async_computation.14 | async-start | bytes 8388608 | tf_op jit(solution)/shard_map/psum | solution.py:205
  969.2 6.5 slice-start.1
  986.8 8.3 copy-start.33
  998.1 6.2 slice-start.3
  1020.8 7.7 copy-start.53
  1035.8 10.7 copy-start.63
  1035.8 10.7 copy-start.79
  1035.8 287.6 %reduce-scatter.5.cloned.1.call-start = ((), (), s32[]{:S(2)}) async-start(), calls=%async_computation.8 | async-start | bytes 7077888 | tf_op jit(solution)/shard_map/reduce_scatter | solution.py:213
  1036.5 10.0 copy-start.5
  1055.2 34.1 %copy-start.34 = (bf16[512,2048]{1,0:T(8,128)(2,1)S(1)}, bf16[512,2048]{1,0:T(8,128)(2,1)}, u32[]{:S(2)}) copy-start(bf16[512,2048]{1,0:T(8,128)(2,1)} %get-tuple-element.78) | copy-start | bytes 6291460
  1265.4 32.8 %copy-start.11 = (bf16[512,2048]{1,0:T(8,128)(2,1)S(1)}, bf16[512,2048]{1,0:T(8,128)(2,1)}, u32[]{:S(2)}) copy-start(bf16[512,2048]{1,0:T(8,128)(2,1)} %copy-done.10) | copy-start | bytes 6291460
  1265.4 32.8 %copy-start.71 = (f32[512]{0:T(512)S(1)}, f32[512]{0:T(512)}, u32[]{:S(2)}) copy-start(f32[512]{0:T(512)} %copy-done.70) | copy-start | bytes 6148
  1265.4 32.8 %copy-start.83 = (f32[512]{0:T(512)S(1)}, f32[512]{0:T(512)}, u32[]{:S(2)}) copy-start(f32[512]{0:T(512)} %copy-done.82) | copy-start | bytes 6148
  1298.2 8.0 copy-start.7
  1298.2 8.0 copy-start.14
  1298.2 8.0 copy-start.20
  1298.3 8.0 copy-start.22
  1298.3 8.0 copy-start.69
  1298.3 8.0 copy-start.81
  (62 other events, 209.3 us)
Sparse Core Ops, SparseCore 0:
  10.5 49.2 all-gather.14
  61.7 28.0 all-gather.16
  94.2 149.5 all-gather.22
  270.6 147.7 all-gather.24
  420.2 52.4 all-gather.18
  474.4 55.8 all-gather.20
  589.9 290.8 all-reduce.14
  911.1 40.1 reduce-scatter.6
  954.8 71.5 reduce-scatter.8
  1029.6 71.7 reduce-scatter.10
  1104.4 155.0 all-reduce.12
  1262.7 60.6 reduce-scatter.4
